TPU v7x, 32 devices: a whole 2x2x4 slice. The times are simulated.
32 devices in a mesh: section: 2 (over core), dp: 8 (over z, x), tensor: 2 (over y).
Axes of the slice: x: 2, y: 2, z: 4, core: 2. Of those that a mesh axis runs over, the one named last changes fastest.
Arguments:
- tokens: bfloat16 [1024, 4096], P('dp', 'tensor'), may hold values from -6 to 6
- gain: bfloat16 [2, 4096], P('section', 'tensor'), may hold values from 0.099609375 to 1.8984375
- w_up: bfloat16 [2, 4096, 5120], P('section', 'dp', 'tensor'), may hold values from -0.09375 to 0.09375
- w_down: bfloat16 [2, 5120, 4096], P('section', 'tensor', 'dp'), may hold values from -0.078125 to 0.078125
- cotangent: bfloat16 [2, 1024, 4096], P('section', 'dp'), may hold values from -6 to 6
Outputs:
- states: bfloat16 [2, 1024, 4096], P('section', 'dp', 'tensor')
- grad_down: bfloat16 [2, 5120, 4096], P('section', 'tensor', 'dp')
All inputs are finite; a program needn't handle non-finite values.
Results may differ from a plain program's by a relative error of at most 0.02.
Values may be sent and summed in bfloat16 or wider, within the bound.
A program may use at most 128 MiB of HBM per device.

v0:
```python
import jax
import jax.numpy as jnp
from jax import lax
from jax.sharding import PartitionSpec as P

EPS = 1e-06
F32 = jnp.float32
BF16 = jnp.bfloat16


def body(tokens, gain, w_up, w_down, cotangent):
    core = lax.axis_index("section")
    layers = lax.axis_size("section")
    assert layers == 2
    dp_id = lax.axis_index("dp")
    dp_count = lax.axis_size("dp")
    tensor_id = lax.axis_index("tensor")
    tensor_count = lax.axis_size("tensor")
    rows, own_width = tokens.shape
    width = own_width * tensor_count
    slice_width = width // dp_count
    hidden_width = w_up.shape[2]
    half = hidden_width // layers
    other = 1 - core
    all_rows = rows * dp_count

    def swap(array):
        return lax.ppermute(array, "section", [(0, 1), (1, 0)])

    def both(own, got):
        return (jnp.where(core == 0, own, got), jnp.where(core == 0, got, own))

    cot_mine = lax.all_to_all(cotangent[0], "dp", split_axis=1, concat_axis=0, tiled=True)
    half_rows = rows // layers
    tok_half = lax.dynamic_slice_in_dim(tokens, core * half_rows, half_rows, 0)
    tok_full = lax.all_gather(tok_half, "tensor", axis=1, tiled=True)
    tok_f = tok_full.astype(F32)
    sums_half = jnp.sum(tok_f * tok_f, axis=1)
    sums_a, sums_b = both(sums_half, swap(sums_half))
    sums = jnp.concatenate([sums_a, sums_b])
    x_half = lax.all_to_all(tok_full, "dp", split_axis=1, concat_axis=0, tiled=True)
    x_a, x_b = both(x_half, swap(x_half))
    x = jnp.concatenate(
        [
            x_a.reshape(dp_count, half_rows, slice_width),
            x_b.reshape(dp_count, half_rows, slice_width),
        ],
        axis=1,
    ).reshape(all_rows, slice_width)
    gain_all = lax.all_gather(gain, "tensor", axis=1, tiled=True)
    gain_own = lax.dynamic_slice_in_dim(gain_all, dp_id * slice_width, slice_width, 1)
    gains = both(gain_own, swap(gain_own))
    up_parts = both(
        lax.dynamic_slice_in_dim(w_up[0], core * half, half, 1),
        swap(lax.dynamic_slice_in_dim(w_up[0], other * half, half, 1)),
    )
    down_parts = both(
        lax.dynamic_slice_in_dim(w_down[0], core * half, half, 0),
        swap(lax.dynamic_slice_in_dim(w_down[0], other * half, half, 0)),
    )
    states = []
    hiddens = []
    for layer in range(layers):
        x_f = x.astype(F32)
        if layer > 0:
            sums = lax.psum_scatter(
                jnp.sum(x_f * x_f, axis=1), "dp", scatter_dimension=0, tiled=True
            )
        scaled = (x_f * gains[layer].astype(F32)).astype(BF16)
        part = jnp.dot(scaled, up_parts[layer], preferred_element_type=F32).astype(BF16)
        pre = lax.psum_scatter(part, "dp", scatter_dimension=0, tiled=True)
        inverse_rms = lax.rsqrt(sums / width + EPS)
        hidden = jax.nn.gelu(pre.astype(F32) * inverse_rms[:, None], approximate=True).astype(BF16)
        hidden_all = lax.all_gather(hidden, "dp", axis=0, tiled=True)
        hiddens.append(hidden_all)
        out = jnp.dot(hidden_all, down_parts[layer], preferred_element_type=F32)
        mid = all_rows // layers
        keep = lax.dynamic_slice_in_dim(out, core * mid, mid, 0)
        give = lax.dynamic_slice_in_dim(out, other * mid, mid, 0).astype(BF16)
        summed = keep + swap(give).astype(F32)
        if tensor_count == 2:
            sent = summed.astype(BF16)
            got = lax.ppermute(sent, "tensor", [(0, 1), (1, 0)])
            summed = sent.astype(F32) + got.astype(F32)
        else:
            summed = lax.psum(summed.astype(BF16), "tensor").astype(F32)
        x_mid = lax.dynamic_slice_in_dim(x_f, core * mid, mid, 0)
        new_mid = (x_mid + summed).astype(BF16)
        new_a, new_b = both(new_mid, swap(new_mid))
        x = jnp.concatenate([new_a, new_b], axis=0)
        states.append(x)
    state_own = jnp.where(core == 0, states[0], states[1])
    state_rows = lax.all_to_all(state_own, "dp", split_axis=0, concat_axis=1, tiled=True)
    state = lax.dynamic_slice_in_dim(state_rows, tensor_id * own_width, own_width, 1)
    hid_keep = jnp.where(core == 0, hiddens[0], hiddens[1])
    hid_got = swap(jnp.where(core == 0, hiddens[1], hiddens[0]))
    hid_parts = both(hid_keep, hid_got)
    hidden_whole = jnp.concatenate(hid_parts, axis=1)
    grad = lax.dot_general(
        hidden_whole, cot_mine, (((0,), (0,)), ((), ())), preferred_element_type=F32
    ).astype(BF16)
    return (state[None], grad[None])


def solution(mesh):
    placed = (
        P("dp", "tensor"),
        P("section", "tensor"),
        P("section", "dp", "tensor"),
        P("section", "tensor", "dp"),
        P("section", "dp", None),
    )
    return jax.shard_map(
        body,
        mesh=mesh,
        in_specs=placed,
        out_specs=(P("section", "dp", "tensor"), P("section", "tensor", "dp")),
        check_vma=False,
    )
```

profile of v0, /device:TPU:0, one launch (start us, length us, event | category | flops | bytes accessed | tf_op | source)
XLA Modules:
  0.0 413.5 jit_solution(5616129061812105178)
XLA Ops:
  7.2 1.0 copy-done
  8.2 10.0 %all_gather.12 = bf16[64,4096]{1,0:T(8,128)(2,1)S(1)} all-gather(bf16[64,2048]{1,0:T(8,128)(2,1)S(1)} %constant_dynamic-slice_fusion.2), channel_id=1, replica_groups=mesh['section'=2,'dp'=8,'tensor'=2] {'tensor'}, dimensions={1}, use_global_device_ids=true | all-gather | bytes 786432 | tf_op jit(solution)/shard_map/all_gather | solution.py:36
  18.2 0.8 copy.22
  19.0 6.2 %all-to-all-start = ((bf16[64,8,512]{2,0,1:T(8,128)(2,1)}), bf16[64,8,512]{2,0,1:T(8,128)(2,1)S(1)}, u32[]{:S(2)}, u32[]{:S(2)}) async-start(bf16[64,8,512]{2,0,1:T(8,128)(2,1)} %bitcast.43), calls=%async_computation | async-start | bytes 1048576 | tf_op jit(solution)/shard_map/all_to_all | solution.py:41
  25.3 2.5 dynamic-slice_bitcast_fusion.1
  27.7 11.2 %all-to-all-done = bf16[64,8,512]{2,0,1:T(8,128)(2,1)S(1)} async-done(((bf16[64,8,512]{2,0,1:T(8,128)(2,1)}), bf16[64,8,512]{2,0,1:T(8,128)(2,1)S(1)}, u32[]{:S(2)}, u32[]{:S(2)}) %all-to-all-start) | async-done | bytes 524320 | tf_op jit(solution)/shard_map/all_to_all | solution.py:41
  38.9 4.3 %all_gather.13 = bf16[1,4096]{1,0:T(2,128)(2,1)S(1)} all-gather(bf16[1,2048]{1,0:T(2,128)(2,1)S(1)} %copy-done.12), channel_id=1, replica_groups=mesh['section'=2,'dp'=8,'tensor'=2] {'tensor'}, dimensions={1}, use_global_device_ids=true | all-gather | bytes 12288 | tf_op jit(solution)/shard_map/all_gather | solution.py:50
  43.3 1.1 collective-permute-done.1
  44.4 0.1 broadcast_select_fusion.9
  44.7 0.3 bitcast_convert_fusion
  45.0 1.4 copy-done.10
  46.4 3.1 convolution_convert_fusion.1
  49.5 0.2 multiply_reduce_fusion.1
  49.7 1.5 collective-permute-start.3
  51.3 0.8 collective-permute-done.3
  52.1 0.1 fusion.48
  52.2 68.8 %reduce-scatter.3.cloned.1.call-done = bf16[128,1280]{1,0:T(8,128)(2,1)} async-done(((bf16[1024,1280]{1,0:T(8,128)(2,1)}), bf16[128,1280]{1,0:T(8,128)(2,1)}) %reduce-scatter.3.cloned.1.call-update) | async-done | bytes 327696 | tf_op jit(solution)/shard_map/reduce_scatter | solution.py:71
  120.9 2.0 fusion.30
  123.0 2.5 dynamic-slice_bitcast_fusion
  125.5 3.4 collective-permute-done.4
  128.9 48.4 %all-gather.3.cloned.1.call-done = bf16[1024,1280]{1,0:T(8,128)(2,1)} async-done(((bf16[128,1280]{1,0:T(8,128)(2,1)}), bf16[1024,1280]{1,0:T(8,128)(2,1)}) %all-gather.3.cloned.1.call-update) | async-done | bytes 2621456 | tf_op jit(solution)/shard_map/all_gather | solution.py:74
  177.3 3.7 fusion.10
  181.0 1.3 copy-done.8
  182.3 0.9 dynamic-slice_convert_fusion.1
  183.1 2.1 collective-permute-done.5
  185.3 1.4 add_convert_fusion.3
  186.7 1.5 collective-permute-start.6
  188.2 12.5 %collective-permute-done.6 = bf16[512,512]{1,0:T(8,128)(2,1)S(1)} collective-permute-done((bf16[512,512]{1,0:T(8,128)(2,1)S(1)}, bf16[512,512]{1,0:T(8,128)(2,1)S(1)}, u32[]{:S(2)}, u32[]{:S(2)}) %collective-permute-start.6) | collective-permute-done | bytes 524320 | tf_op jit(solution)/shard_map/ppermute | solution.py:83
  200.7 0.2 add_convert_fusion.2
  201.0 1.9 collective-permute-done.7
  202.9 0.1 broadcast_select_fusion.7
  203.0 4.8 %convolution_convert_fusion = bf16[1024,1280]{1,0:T(8,128)(2,1)} fusion(bf16[512,1280]{1,0:T(8,128)(2,1)} %collective-permute-done.2, pred[]{:T(512)S(6)} %eq.2, bf16[1,512,2560]{2,1,0:T(8,128)(2,1)S(1)} %copy-done.11, s32[]{:T(128)S(6)} %select_n.145, f32[512]{0:T(512)S(1)} %bitcast.52, bf16[512,512]{1,0:T(8,128)(2,1)S(1)} %get-tuple-element.7, ...), kind=kOutput, calls=%fused_computation.6 | convolution fusion | flops 1347289088 | bytes 6293509 | tf_op jit(solution)/shard_map/dot_general | solution.py:70
  207.8 0.6 copy-done.13
  208.4 0.6 dynamic-slice.4
  209.7 0.3 multiply_reduce_fusion
  209.9 19.5 %all-reduce = f32[1024]{0:T(1024)S(1)} all-reduce(f32[1024]{0:T(1024)S(1)} %multiply_reduce_fusion), channel_id=4, replica_groups=mesh['section'=2,'dp'=8,'tensor'=2] {'dp'}, use_global_device_ids=true, to_apply=%region_4.5.clone | all-reduce | flops 1024 | bytes 8192
  229.5 0.1 fusion.47
  229.5 48.0 %reduce-scatter.5.cloned.1.call-done = bf16[128,1280]{1,0:T(8,128)(2,1)} async-done(((bf16[1024,1280]{1,0:T(8,128)(2,1)}), bf16[128,1280]{1,0:T(8,128)(2,1)}) %reduce-scatter.5.cloned.1.call-update) | async-done | bytes 327696 | tf_op jit(solution)/shard_map/reduce_scatter | solution.py:71
  277.5 2.0 fusion.38
  279.5 54.1 %all-gather.5.cloned.1.call-done = bf16[1024,1280]{1,0:T(8,128)(2,1)} async-done(((bf16[128,1280]{1,0:T(8,128)(2,1)}), bf16[1024,1280]{1,0:T(8,128)(2,1)}) %all-gather.5.cloned.1.call-update) | async-done | bytes 2621456 | tf_op jit(solution)/shard_map/all_gather | solution.py:74
  333.7 4.2 %fusion.11 = f32[1024,512]{1,0:T(8,128)S(1)} fusion(bf16[1024,1280]{1,0:T(8,128)(2,1)} %all-gather.5.cloned.1.call-done, bf16[1280,512]{1,0:T(8,128)(2,1)} %collective-permute-done.4, pred[]{:T(512)S(6)} %eq.2, bf16[1,2560,512]{2,1,0:T(8,128)(2,1)} %param.8, s32[]{:T(128)S(6)} %select_n.145), kind=kOutput, calls=%fused_computation.18 | convolution fusion | flops 1342832640 | bytes 7340037 | tf_op jit(solution)/shard_map/dot_general | solution.py:76
  337.9 1.3 copy-done.7
  339.2 0.9 dynamic-slice_convert_fusion
  340.0 1.8 broadcast_select_fusion.2
  341.9 0.5 collective-permute-start.11
  342.4 2.3 copy.18
  344.7 4.2 %all-to-all-start.2 = ((bf16[128,8,512]{0,2,1:T(8,128)(2,1)}), bf16[128,8,512]{0,2,1:T(8,128)(2,1)}, u32[]{:S(2)}, u32[]{:S(2)}) async-start(bf16[128,8,512]{0,2,1:T(8,128)(2,1)} %bitcast.45), calls=%async_computation.4 | async-start | bytes 2097152 | tf_op jit(solution)/shard_map/all_to_all | solution.py:33
  348.9 1.6 add_convert_fusion.1
  350.6 1.5 collective-permute-start.9
  352.1 0.3 fusion.50
  352.4 12.1 %collective-permute-done.9 = bf16[512,512]{1,0:T(8,128)(2,1)S(1)} collective-permute-done((bf16[512,512]{1,0:T(8,128)(2,1)S(1)}, bf16[512,512]{1,0:T(8,128)(2,1)S(1)}, u32[]{:S(2)}, u32[]{:S(2)}) %collective-permute-start.9) | collective-permute-done | bytes 524320 | tf_op jit(solution)/shard_map/ppermute | solution.py:83
  364.5 0.2 add_convert_fusion
  364.8 1.9 collective-permute-done.10
  366.7 0.1 broadcast_select_fusion.5
  366.8 1.2 maximum_select_fusion
  368.0 2.3 copy.16
  370.3 4.8 %all-to-all-done.2 = bf16[128,8,512]{0,2,1:T(8,128)(2,1)} async-done(((bf16[128,8,512]{0,2,1:T(8,128)(2,1)}), bf16[128,8,512]{0,2,1:T(8,128)(2,1)}, u32[]{:S(2)}, u32[]{:S(2)}) %all-to-all-start.2) | async-done | bytes 1048608 | tf_op jit(solution)/shard_map/all_to_all | solution.py:33
  375.1 4.4 %all-to-all-start.1 = ((bf16[8,128,512]{1,2,0:T(8,128)(2,1)}), bf16[8,128,512]{1,2,0:T(8,128)(2,1)}, u32[]{:S(2)}, u32[]{:S(2)}) async-start(bf16[8,128,512]{1,2,0:T(8,128)(2,1)} %copy.16), calls=%async_computation.3 | async-start | bytes 2097152 | tf_op jit(solution)/shard_map/all_to_all | solution.py:93
  379.6 2.3 copy.19
  381.8 2.3 broadcast_select_fusion.1
  384.1 4.3 %fusion.7 = bf16[1,2560,512]{2,1,0:T(8,128)(2,1)} fusion(bf16[1024,512]{1,0:T(8,128)(2,1)S(1)} %bitcast.50, bf16[1024,1280]{1,0:T(8,128)(2,1)S(1)} %get-tuple-element.3, bf16[1024,1280]{1,0:T(8,128)(2,1)S(1)} %get-tuple-element.2), kind=kOutput, calls=%fused_computation.5 | convolution fusion | flops 2696151040 | bytes 8912896 | tf_op jit(solution)/shard_map/dot_general | solution.py:99
  388.4 16.5 %all-to-all-done.1 = bf16[8,128,512]{1,2,0:T(8,128)(2,1)} async-done(((bf16[8,128,512]{1,2,0:T(8,128)(2,1)}), bf16[8,128,512]{1,2,0:T(8,128)(2,1)}, u32[]{:S(2)}, u32[]{:S(2)}) %all-to-all-start.1) | async-done | bytes 1048608 | tf_op jit(solution)/shard_map/all_to_all | solution.py:93
  404.9 1.1 constant_dynamic-slice_fusion
  405.9 1.0 copy.17
  (48 shorter events, 0.6 us)
Async XLA Ops:
  7.2 1.0 copy-start
  19.0 19.8 %copy-start.12 = (bf16[1,2048]{1,0:T(2,128)(2,1)S(1)}, bf16[1,2048]{1,0:T(2,128)(2,1)}, u32[]{:S(2)}) copy-start(bf16[1,2048]{1,0:T(2,128)(2,1)} %param.6) | copy-start | bytes 12292
  19.0 19.8 %all-to-all-start = ((bf16[64,8,512]{2,0,1:T(8,128)(2,1)}), bf16[64,8,512]{2,0,1:T(8,128)(2,1)S(1)}, u32[]{:S(2)}, u32[]{:S(2)}) async-start(bf16[64,8,512]{2,0,1:T(8,128)(2,1)} %bitcast.43), calls=%async_computation | async-start | bytes 1048576 | tf_op jit(solution)/shard_map/all_to_all | solution.py:41
  25.2 95.7 %reduce-scatter.3.cloned.1.call-start = ((), (), s32[]{:S(2)}) async-start(), calls=%async_computation.5 | async-start | bytes 2949120 | tf_op jit(solution)/shard_map/reduce_scatter | solution.py:71
  27.7 17.3 %collective-permute-start.2 = (bf16[512,1280]{1,0:T(8,128)(2,1)}, bf16[512,1280]{1,0:T(8,128)(2,1)}, u32[]{:S(2)}, u32[]{:S(2)}) collective-permute-start(bf16[512,1280]{1,0:T(8,128)(2,1)} %dynamic-slice_bitcast_fusion.1), channel_id=1, source_target_pairs={{0,16},{16,0},{1,17},{17,1},{2,18},{18,2},{3,19},{19,3},{4,20},{20... | collective-permute-start | bytes 3932168 | tf_op jit(solution)/shard_map/ppermute | solution.py:28
  38.9 5.6 %collective-permute-start = (bf16[512,512]{1,0:T(8,128)(2,1)S(1)}, bf16[512,512]{1,0:T(8,128)(2,1)S(1)}, u32[]{:S(2)}, u32[]{:S(2)}) collective-permute-start(bf16[512,512]{1,0:T(8,128)(2,1)S(1)} %bitcast.47), channel_id=1, source_target_pairs={{0,16},{16,0},{1,17},{17,1},{2,18},{18,2},{3,19},{19,3},{4,20},{20... | collective-permute-start | bytes 1572872 | tf_op jit(solution)/shard_map/ppermute | solution.py:28
  43.2 1.2 collective-permute-start.1
  44.6 1.7 copy-start.10
  49.5 127.8 %all-gather.3.cloned.1.call-start = ((), (), s32[]{:S(2)}) async-start(), calls=%async_computation.6 | async-start | bytes 2949120 | tf_op jit(solution)/shard_map/all_gather | solution.py:74
  49.7 2.3 collective-permute-start.3
  123.0 154.5 %reduce-scatter.5.cloned.1.call-start = ((), (), s32[]{:S(2)}) async-start(), calls=%async_computation.7 | async-start | bytes 2949120 | tf_op jit(solution)/shard_map/reduce_scatter | solution.py:71
  125.5 3.4 collective-permute-start.4
  180.9 1.3 copy-start.8
  183.1 2.1 collective-permute-start.5
  186.6 16.3 %copy-start.11 = (bf16[1,512,2560]{2,1,0:T(8,128)(2,1)S(1)}, bf16[1,512,2560]{2,1,0:T(8,128)(2,1)}, u32[]{:S(2)}) copy-start(bf16[1,512,2560]{2,1,0:T(8,128)(2,1)} %param.7) | copy-start | bytes 7864324
  186.7 14.0 %collective-permute-start.6 = (bf16[512,512]{1,0:T(8,128)(2,1)S(1)}, bf16[512,512]{1,0:T(8,128)(2,1)S(1)}, u32[]{:S(2)}, u32[]{:S(2)}) collective-permute-start(bf16[512,512]{1,0:T(8,128)(2,1)S(1)} %add_convert_fusion.3), channel_id=1, source_target_pairs={{0,1},{1,0},{2,3},{3,2},{4,5},{5,4},{6,7},{7,6},{8,9},{9,8},{10,11... | collective-permute-start | bytes 1572872 | tf_op jit(solution)/shard_map/ppermute | solution.py:83
  200.9 2.0 collective-permute-start.7
  203.0 6.7 %copy-start.3 = (bf16[512,512]{1,0:T(8,128)(2,1)}, bf16[512,512]{1,0:T(8,128)(2,1)S(1)}, u32[]{:S(2)}) copy-start(bf16[512,512]{1,0:T(8,128)(2,1)S(1)} %get-tuple-element.6) | copy-start | bytes 1572868
  203.0 6.7 %copy-start.5 = (bf16[512,512]{1,0:T(8,128)(2,1)}, bf16[512,512]{1,0:T(8,128)(2,1)S(1)}, u32[]{:S(2)}) copy-start(bf16[512,512]{1,0:T(8,128)(2,1)S(1)} %get-tuple-element.7) | copy-start | bytes 1572868
  207.7 0.7 copy-start.13
  207.8 125.9 %all-gather.5.cloned.1.call-start = ((), (), s32[]{:S(2)}) async-start(), calls=%async_computation.8 | async-start | bytes 2949120 | tf_op jit(solution)/shard_map/all_gather | solution.py:74
  333.6 6.4 %copy-start.1 = (bf16[1024,1280]{1,0:T(8,128)(2,1)S(1)}, bf16[1024,1280]{1,0:T(8,128)(2,1)}, u32[]{:S(2)}) copy-start(bf16[1024,1280]{1,0:T(8,128)(2,1)} %all-gather.3.cloned.1.call-done) | copy-start | bytes 7864324
  333.6 6.4 %copy-start.2 = (bf16[1024,1280]{1,0:T(8,128)(2,1)S(1)}, bf16[1024,1280]{1,0:T(8,128)(2,1)}, u32[]{:S(2)}) copy-start(bf16[1024,1280]{1,0:T(8,128)(2,1)} %all-gather.5.cloned.1.call-done) | copy-start | bytes 7864324
  337.8 1.3 copy-start.7
  340.0 8.9 %collective-permute-start.8 = (bf16[512,512]{1,0:T(8,128)(2,1)}, bf16[512,512]{1,0:T(8,128)(2,1)}, u32[]{:S(2)}, u32[]{:S(2)}) collective-permute-start(bf16[512,512]{1,0:T(8,128)(2,1)} %dynamic-slice_convert_fusion), channel_id=1, source_target_pairs={{0,16},{16,0},{1,17},{17,1},{2,18},{18,2},{3,19},{19,3},{4,20},{20... | collective-permute-start | bytes 1572872 | tf_op jit(solution)/shard_map/ppermute | solution.py:28
  341.9 40.0 %collective-permute-start.11 = (bf16[1024,1280]{1,0:T(8,128)(2,1)}, bf16[1024,1280]{1,0:T(8,128)(2,1)}, u32[]{:S(2)}, u32[]{:S(2)}) collective-permute-start(bf16[1024,1280]{1,0:T(8,128)(2,1)} %broadcast_select_fusion.2), channel_id=1, source_target_pairs={{0,16},{16,0},{1,17},{17,1},{2,18},{18,2},{3,19},{19,3},{4,20},{20... | collective-permute-start | bytes 7864328 | tf_op jit(solution)/shard_map/ppermute | solution.py:28
  344.7 30.5 %all-to-all-start.2 = ((bf16[128,8,512]{0,2,1:T(8,128)(2,1)}), bf16[128,8,512]{0,2,1:T(8,128)(2,1)}, u32[]{:S(2)}, u32[]{:S(2)}) async-start(bf16[128,8,512]{0,2,1:T(8,128)(2,1)} %bitcast.45), calls=%async_computation.4 | async-start | bytes 2097152 | tf_op jit(solution)/shard_map/all_to_all | solution.py:33
  348.9 3.2 copy-start.4
  348.9 3.2 copy-start.6
  350.6 13.9 %collective-permute-start.9 = (bf16[512,512]{1,0:T(8,128)(2,1)S(1)}, bf16[512,512]{1,0:T(8,128)(2,1)S(1)}, u32[]{:S(2)}, u32[]{:S(2)}) collective-permute-start(bf16[512,512]{1,0:T(8,128)(2,1)S(1)} %add_convert_fusion.1), channel_id=1, source_target_pairs={{0,1},{1,0},{2,3},{3,2},{4,5},{5,4},{6,7},{7,6},{8,9},{9,8},{10,11... | collective-permute-start | bytes 1572872 | tf_op jit(solution)/shard_map/ppermute | solution.py:83
  364.7 2.0 collective-permute-start.10
  375.1 29.8 %all-to-all-start.1 = ((bf16[8,128,512]{1,2,0:T(8,128)(2,1)}), bf16[8,128,512]{1,2,0:T(8,128)(2,1)}, u32[]{:S(2)}, u32[]{:S(2)}) async-start(bf16[8,128,512]{1,2,0:T(8,128)(2,1)} %copy.16), calls=%async_computation.3 | async-start | bytes 2097152 | tf_op jit(solution)/shard_map/all_to_all | solution.py:93
  381.8 2.3 copy-start.9
Sparse Core Ops, SparseCore 0:
  49.6 71.2 reduce-scatter.2
  123.7 53.5 all-gather.2
  207.9 69.5 reduce-scatter.4
  280.1 53.4 all-gather.4
where the time goes:
time: 414 us; the launch traced here: 413 us
  waiting for transfers between devices  288 us (70%)
  blocking collectives  33.8 us (8%)
  local copies, waits for them, and re-layouts  22.6 us (5%)
  starting transfers between devices  20.3 us (5%)
  matrix products  20 us (5%)
  between operations  14.7 us (4%)
  other arithmetic  14.5 us (4%)
    reduce_scatter x2, waiting for transfers between devices, body(): pre = lax.psum_scatter(part, 'dp', scatter_dimension=0, tiled=True)  117 us
    all_gather x2, waiting for transfers between devices, body(): hidden_all = lax.all_gather(hidden, 'dp', axis=0, tiled=True)  103 us
    ppermute x2, waiting for transfers between devices, body(): got = lax.ppermute(sent, 'tensor', [(0, 1), (1, 0)])  24.6 us
    unnamed x1, blocking collectives  19.5 us
    all_to_all x1, waiting for transfers between devices, body(): lax.all_to_all(state_own, 'dp', split_axis=0, concat_axis=1, tiled=True)  16.5 us
    ppermute x10, waiting for transfers between devices, swap(): return lax.ppermute(array, 'section', [(0, 1), (1, 0)])  11.3 us
    all_to_all x1, waiting for transfers between devices, body(): lax.all_to_all(tok_full, 'dp', split_axis=1, concat_axis=0, tiled=True)  11.2 us
    all_gather x1, blocking collectives, body(): tok_full = lax.all_gather(tok_half, 'tensor', axis=1, tiled=True)  9.97 us
  transfers between devices with their start and end apart: 19, of which 15 were waited for; matrix products, arithmetic and copies ran while one was open for 6% of the time, Pallas kernels for 0%

commit v1 on v0

--- a/solution.py
+++ b/solution.py
@@ -90,7 +90,9 @@
         x = jnp.concatenate([new_a, new_b], axis=0)
         states.append(x)
     state_own = jnp.where(core == 0, states[0], states[1])
-    state_rows = lax.all_to_all(state_own, "dp", split_axis=0, concat_axis=1, tiled=True)
+    state_rows = jnp.concatenate(
+        jax.lax.all_to_all(jnp.stack(jnp.split(state_own, jax.lax.psum(1, "dp"), 0)), "dp", 0, 0), 1
+    )
     state = lax.dynamic_slice_in_dim(state_rows, tensor_id * own_width, own_width, 1)
     hid_keep = jnp.where(core == 0, hiddens[0], hiddens[1])
     hid_got = swap(jnp.where(core == 0, hiddens[1], hiddens[0]))

time: 414 us -> 430 us (1.039)
  waiting for transfers between devices: 288 us -> 302 us
    all_to_all x1, waiting for transfers between devices: 4.83 us -> 19.1 us  [body(): lax.all_to_all(cotangent[0], 'dp', split_axis=1, concat_axis=0, tiled=True)]
    unnamed x30 -> x35, local copies, waits for them, and re-layouts: 8.5 us -> 11.9 us
where the time goes in v1:
time: 430 us; the launch traced here: 429 us
  waiting for transfers between devices  302 us (70%)
  blocking collectives  33.8 us (8%)
  local copies, waits for them, and re-layouts  24.3 us (6%)
  starting transfers between devices  20.3 us (5%)
  matrix products  19.8 us (5%)
  between operations  14.7 us (3%)
  other arithmetic  14.1 us (3%)
    reduce_scatter x2, waiting for transfers between devices, body(): pre = lax.psum_scatter(part, 'dp', scatter_dimension=0, tiled=True)  117 us
    all_gather x2, waiting for transfers between devices, body(): hidden_all = lax.all_gather(hidden, 'dp', axis=0, tiled=True)  103 us
    ppermute x2, waiting for transfers between devices, body(): got = lax.ppermute(sent, 'tensor', [(0, 1), (1, 0)])  24.7 us
    unnamed x1, blocking collectives  19.5 us
    all_to_all x1, waiting for transfers between devices, body(): lax.all_to_all(cotangent[0], 'dp', split_axis=1, concat_axis=0, tiled=True)  19.1 us
    all_to_all x1, waiting for transfers between devices, body(): jax.lax.all_to_all(jnp.stack(jnp.split(state_own, jax.lax.psum(1, 'dp'),...  16.4 us
    unnamed x35, local copies, waits for them, and re-layouts  11.9 us
    ppermute x10, waiting for transfers between devices, swap(): return lax.ppermute(array, 'section', [(0, 1), (1, 0)])  11.3 us
  transfers between devices with their start and end apart: 19, of which 15 were waited for; matrix products, arithmetic and copies ran while one was open for 6% of the time, Pallas kernels for 0%

profile of v1, /device:TPU:0, one launch (start us, length us, event | category | flops | bytes accessed | tf_op | source)
XLA Modules:
  0.0 429.0 jit_solution(96624576552657300)
XLA Ops:
  7.2 1.0 copy-done
  8.2 10.0 %all_gather.12 = bf16[64,4096]{1,0:T(8,128)(2,1)S(1)} all-gather(bf16[64,2048]{1,0:T(8,128)(2,1)S(1)} %constant_dynamic-slice_fusion.2), channel_id=1, replica_groups=mesh['section'=2,'dp'=8,'tensor'=2] {'tensor'}, dimensions={1}, use_global_device_ids=true | all-gather | bytes 786432 | tf_op jit(solution)/shard_map/all_gather | solution.py:36
  18.2 0.8 copy.22
  19.0 6.2 %all-to-all-start = ((bf16[64,8,512]{2,0,1:T(8,128)(2,1)}), bf16[64,8,512]{2,0,1:T(8,128)(2,1)S(1)}, u32[]{:S(2)}, u32[]{:S(2)}) async-start(bf16[64,8,512]{2,0,1:T(8,128)(2,1)} %bitcast.73), calls=%async_computation | async-start | bytes 1048576 | tf_op jit(solution)/shard_map/all_to_all | solution.py:41
  25.3 2.5 dynamic-slice_bitcast_fusion.1
  27.7 11.2 %all-to-all-done = bf16[64,8,512]{2,0,1:T(8,128)(2,1)S(1)} async-done(((bf16[64,8,512]{2,0,1:T(8,128)(2,1)}), bf16[64,8,512]{2,0,1:T(8,128)(2,1)S(1)}, u32[]{:S(2)}, u32[]{:S(2)}) %all-to-all-start) | async-done | bytes 524320 | tf_op jit(solution)/shard_map/all_to_all | solution.py:41
  38.9 4.3 %all_gather.13 = bf16[1,4096]{1,0:T(2,128)(2,1)S(1)} all-gather(bf16[1,2048]{1,0:T(2,128)(2,1)S(1)} %copy-done.11), channel_id=1, replica_groups=mesh['section'=2,'dp'=8,'tensor'=2] {'tensor'}, dimensions={1}, use_global_device_ids=true | all-gather | bytes 12288 | tf_op jit(solution)/shard_map/all_gather | solution.py:50
  43.3 1.1 collective-permute-done.1
  44.7 0.3 bitcast_convert_fusion
  45.0 1.4 copy-done.9
  46.4 3.1 convolution_convert_fusion.1
  49.5 0.2 multiply_reduce_fusion.1
  49.7 1.5 collective-permute-start.3
  51.3 0.8 collective-permute-done.3
  52.2 68.8 %reduce-scatter.3.cloned.1.call-done = bf16[128,1280]{1,0:T(8,128)(2,1)} async-done(((bf16[1024,1280]{1,0:T(8,128)(2,1)}), bf16[128,1280]{1,0:T(8,128)(2,1)}) %reduce-scatter.3.cloned.1.call-update) | async-done | bytes 327696 | tf_op jit(solution)/shard_map/reduce_scatter | solution.py:71
  120.9 2.0 fusion.30
  123.0 2.5 dynamic-slice_bitcast_fusion
  125.5 3.4 collective-permute-done.4
  128.9 48.4 %all-gather.3.cloned.1.call-done = bf16[1024,1280]{1,0:T(8,128)(2,1)} async-done(((bf16[128,1280]{1,0:T(8,128)(2,1)}), bf16[1024,1280]{1,0:T(8,128)(2,1)}) %all-gather.3.cloned.1.call-update) | async-done | bytes 2621456 | tf_op jit(solution)/shard_map/all_gather | solution.py:74
  177.3 3.7 fusion.10
  181.0 1.3 copy-done.7
  182.3 0.9 dynamic-slice_convert_fusion.1
  183.1 2.1 collective-permute-done.5
  185.3 1.4 add_convert_fusion.3
  186.7 1.5 collective-permute-start.6
  188.2 12.5 %collective-permute-done.6 = bf16[512,512]{1,0:T(8,128)(2,1)S(1)} collective-permute-done((bf16[512,512]{1,0:T(8,128)(2,1)S(1)}, bf16[512,512]{1,0:T(8,128)(2,1)S(1)}, u32[]{:S(2)}, u32[]{:S(2)}) %collective-permute-start.6) | collective-permute-done | bytes 524320 | tf_op jit(solution)/shard_map/ppermute | solution.py:83
  200.7 0.2 add_convert_fusion.2
  201.0 1.9 collective-permute-done.7
  203.0 4.8 %convolution_convert_fusion = bf16[1024,1280]{1,0:T(8,128)(2,1)} fusion(bf16[512,1280]{1,0:T(8,128)(2,1)} %collective-permute-done.2, pred[]{:T(512)S(6)} %eq.2, bf16[1,512,2560]{2,1,0:T(8,128)(2,1)S(1)} %copy-done.10, s32[]{:T(128)S(6)} %select_n.141, f32[512]{0:T(512)S(1)} %bitcast.82, bf16[512,512]{1,0:T(8,128)(2,1)S(1)} %get-tuple-element.7, ...), kind=kOutput, calls=%fused_computation.6 | convolution fusion | flops 1347289088 | bytes 6293509 | tf_op jit(solution)/shard_map/dot_general | solution.py:70
  207.8 0.6 copy-done.12
  208.4 0.6 dynamic-slice.4
  209.6 0.3 multiply_reduce_fusion
  209.9 19.5 %all-reduce = f32[1024]{0:T(1024)S(1)} all-reduce(f32[1024]{0:T(1024)S(1)} %multiply_reduce_fusion), channel_id=4, replica_groups=mesh['section'=2,'dp'=8,'tensor'=2] {'dp'}, use_global_device_ids=true, to_apply=%region_4.5.clone | all-reduce | flops 1024 | bytes 8192
  229.5 48.0 %reduce-scatter.5.cloned.1.call-done = bf16[128,1280]{1,0:T(8,128)(2,1)} async-done(((bf16[1024,1280]{1,0:T(8,128)(2,1)}), bf16[128,1280]{1,0:T(8,128)(2,1)}) %reduce-scatter.5.cloned.1.call-update) | async-done | bytes 327696 | tf_op jit(solution)/shard_map/reduce_scatter | solution.py:71
  277.5 2.0 fusion.38
  279.6 54.1 %all-gather.5.cloned.1.call-done = bf16[1024,1280]{1,0:T(8,128)(2,1)} async-done(((bf16[128,1280]{1,0:T(8,128)(2,1)}), bf16[1024,1280]{1,0:T(8,128)(2,1)}) %all-gather.5.cloned.1.call-update) | async-done | bytes 2621456 | tf_op jit(solution)/shard_map/all_gather | solution.py:74
  333.7 4.0 fusion.11
  337.9 1.9 collective-permute-done.8
  340.0 1.5 collective-permute-start.9
  341.5 0.3 fusion.58
  341.8 12.2 %collective-permute-done.9 = bf16[512,512]{1,0:T(8,128)(2,1)S(1)} collective-permute-done((bf16[512,512]{1,0:T(8,128)(2,1)S(1)}, bf16[512,512]{1,0:T(8,128)(2,1)S(1)}, u32[]{:S(2)}, u32[]{:S(2)}) %collective-permute-start.9) | collective-permute-done | bytes 524320 | tf_op jit(solution)/shard_map/ppermute | solution.py:83
  354.0 1.0 add_convert_fusion
  355.0 1.8 broadcast_select_fusion.2
  356.8 0.5 collective-permute-start.11
  357.3 2.3 copy.18
  359.6 4.3 all-to-all-start.2
  363.9 1.4 broadcast_select_fusion.5
  365.4 0.3 maximum_select_fusion
  365.7 0.7 fusion.46
  366.3 0.7 fusion.45
  367.0 0.7 fusion.44
  367.7 0.7 fusion.43
  368.3 0.7 fusion.42
  369.0 0.7 fusion.41
  369.7 0.7 fusion.40
  370.3 0.6 fusion.39
  371.0 19.1 %all-to-all-done.2 = bf16[128,8,512]{0,2,1:T(8,128)(2,1)} async-done(((bf16[128,8,512]{0,2,1:T(8,128)(2,1)}), bf16[128,8,512]{0,2,1:T(8,128)(2,1)}, u32[]{:S(2)}, u32[]{:S(2)}) %all-to-all-start.2) | async-done | bytes 1048608 | tf_op jit(solution)/shard_map/all_to_all | solution.py:33
  390.1 4.4 %all-to-all-start.1 = ((bf16[8,128,512]{2,1,0:T(8,128)(2,1)}), bf16[8,128,512]{2,1,0:T(8,128)(2,1)}, u32[]{:S(2)}, u32[]{:S(2)}) async-start(bf16[8,128,512]{2,1,0:T(8,128)(2,1)} %fusion.39), calls=%async_computation.3 | async-start | bytes 2097152 | tf_op jit(solution)/shard_map/all_to_all | solution.py:94
  394.5 2.3 copy.19
  396.9 2.3 broadcast_select_fusion.1
  399.2 4.3 fusion.7
  403.4 16.4 %all-to-all-done.1 = bf16[8,128,512]{2,1,0:T(8,128)(2,1)} async-done(((bf16[8,128,512]{2,1,0:T(8,128)(2,1)}), bf16[8,128,512]{2,1,0:T(8,128)(2,1)}, u32[]{:S(2)}, u32[]{:S(2)}) %all-to-all-start.1) | async-done | bytes 1048608 | tf_op jit(solution)/shard_map/all_to_all | solution.py:94
  419.8 1.6 copy.16
  421.5 1.0 copy.17
  (54 shorter events, 1.3 us)
Async XLA Ops:
  7.2 1.0 copy-start
  19.0 19.8 %copy-start.11 = (bf16[1,2048]{1,0:T(2,128)(2,1)S(1)}, bf16[1,2048]{1,0:T(2,128)(2,1)}, u32[]{:S(2)}) copy-start(bf16[1,2048]{1,0:T(2,128)(2,1)} %param.6) | copy-start | bytes 12292
  19.0 19.8 %all-to-all-start = ((bf16[64,8,512]{2,0,1:T(8,128)(2,1)}), bf16[64,8,512]{2,0,1:T(8,128)(2,1)S(1)}, u32[]{:S(2)}, u32[]{:S(2)}) async-start(bf16[64,8,512]{2,0,1:T(8,128)(2,1)} %bitcast.73), calls=%async_computation | async-start | bytes 1048576 | tf_op jit(solution)/shard_map/all_to_all | solution.py:41
  25.2 95.7 %reduce-scatter.3.cloned.1.call-start = ((), (), s32[]{:S(2)}) async-start(), calls=%async_computation.5 | async-start | bytes 2949120 | tf_op jit(solution)/shard_map/reduce_scatter | solution.py:71
  27.7 17.3 %collective-permute-start.2 = (bf16[512,1280]{1,0:T(8,128)(2,1)}, bf16[512,1280]{1,0:T(8,128)(2,1)}, u32[]{:S(2)}, u32[]{:S(2)}) collective-permute-start(bf16[512,1280]{1,0:T(8,128)(2,1)} %dynamic-slice_bitcast_fusion.1), channel_id=1, source_target_pairs={{0,16},{16,0},{1,17},{17,1},{2,18},{18,2},{3,19},{19,3},{4,20},{20... | collective-permute-start | bytes 3932168 | tf_op jit(solution)/shard_map/ppermute | solution.py:28
  38.9 5.6 %collective-permute-start = (bf16[512,512]{1,0:T(8,128)(2,1)S(1)}, bf16[512,512]{1,0:T(8,128)(2,1)S(1)}, u32[]{:S(2)}, u32[]{:S(2)}) collective-permute-start(bf16[512,512]{1,0:T(8,128)(2,1)S(1)} %bitcast.77), channel_id=1, source_target_pairs={{0,16},{16,0},{1,17},{17,1},{2,18},{18,2},{3,19},{19,3},{4,20},{20... | collective-permute-start | bytes 1572872 | tf_op jit(solution)/shard_map/ppermute | solution.py:28
  43.2 1.2 collective-permute-start.1
  44.6 1.7 copy-start.9
  49.5 127.8 %all-gather.3.cloned.1.call-start = ((), (), s32[]{:S(2)}) async-start(), calls=%async_computation.6 | async-start | bytes 2949120 | tf_op jit(solution)/shard_map/all_gather | solution.py:74
  49.7 2.3 collective-permute-start.3
  123.0 154.5 %reduce-scatter.5.cloned.1.call-start = ((), (), s32[]{:S(2)}) async-start(), calls=%async_computation.7 | async-start | bytes 2949120 | tf_op jit(solution)/shard_map/reduce_scatter | solution.py:71
  125.5 3.4 collective-permute-start.4
  180.9 1.3 copy-start.7
  183.1 2.1 collective-permute-start.5
  186.6 16.3 %copy-start.10 = (bf16[1,512,2560]{2,1,0:T(8,128)(2,1)S(1)}, bf16[1,512,2560]{2,1,0:T(8,128)(2,1)}, u32[]{:S(2)}) copy-start(bf16[1,512,2560]{2,1,0:T(8,128)(2,1)} %param.7) | copy-start | bytes 7864324
  186.7 14.0 %collective-permute-start.6 = (bf16[512,512]{1,0:T(8,128)(2,1)S(1)}, bf16[512,512]{1,0:T(8,128)(2,1)S(1)}, u32[]{:S(2)}, u32[]{:S(2)}) collective-permute-start(bf16[512,512]{1,0:T(8,128)(2,1)S(1)} %add_convert_fusion.3), channel_id=1, source_target_pairs={{0,1},{1,0},{2,3},{3,2},{4,5},{5,4},{6,7},{7,6},{8,9},{9,8},{10,11... | collective-permute-start | bytes 1572872 | tf_op jit(solution)/shard_map/ppermute | solution.py:83
  200.9 2.0 collective-permute-start.7
  203.0 138.5 %copy-start.3 = (bf16[512,512]{1,0:T(8,128)(2,1)}, bf16[512,512]{1,0:T(8,128)(2,1)S(1)}, u32[]{:S(2)}) copy-start(bf16[512,512]{1,0:T(8,128)(2,1)S(1)} %get-tuple-element.6) | copy-start | bytes 1572868
  203.0 138.5 %copy-start.5 = (bf16[512,512]{1,0:T(8,128)(2,1)}, bf16[512,512]{1,0:T(8,128)(2,1)S(1)}, u32[]{:S(2)}) copy-start(bf16[512,512]{1,0:T(8,128)(2,1)S(1)} %get-tuple-element.7) | copy-start | bytes 1572868
  207.7 0.7 copy-start.12
  207.8 125.9 %all-gather.5.cloned.1.call-start = ((), (), s32[]{:S(2)}) async-start(), calls=%async_computation.8 | async-start | bytes 2949120 | tf_op jit(solution)/shard_map/all_gather | solution.py:74
  337.8 2.0 collective-permute-start.8
  340.0 14.0 %collective-permute-start.9 = (bf16[512,512]{1,0:T(8,128)(2,1)S(1)}, bf16[512,512]{1,0:T(8,128)(2,1)S(1)}, u32[]{:S(2)}, u32[]{:S(2)}) collective-permute-start(bf16[512,512]{1,0:T(8,128)(2,1)S(1)} %add_convert_fusion.1), channel_id=1, source_target_pairs={{0,1},{1,0},{2,3},{3,2},{4,5},{5,4},{6,7},{7,6},{8,9},{9,8},{10,11... | collective-permute-start | bytes 1572872 | tf_op jit(solution)/shard_map/ppermute | solution.py:83
  341.5 13.5 %copy-start.2 = (bf16[1024,1280]{1,0:T(8,128)(2,1)S(1)}, bf16[1024,1280]{1,0:T(8,128)(2,1)}, u32[]{:S(2)}) copy-start(bf16[1024,1280]{1,0:T(8,128)(2,1)} %all-gather.5.cloned.1.call-done) | copy-start | bytes 7864324
  341.8 13.2 %copy-start.1 = (bf16[1024,1280]{1,0:T(8,128)(2,1)S(1)}, bf16[1024,1280]{1,0:T(8,128)(2,1)}, u32[]{:S(2)}) copy-start(bf16[1024,1280]{1,0:T(8,128)(2,1)} %all-gather.3.cloned.1.call-done) | copy-start | bytes 7864324
  355.0 8.9 %collective-permute-start.10 = (bf16[512,512]{1,0:T(8,128)(2,1)}, bf16[512,512]{1,0:T(8,128)(2,1)}, u32[]{:S(2)}, u32[]{:S(2)}) collective-permute-start(bf16[512,512]{1,0:T(8,128)(2,1)} %add_convert_fusion), channel_id=1, source_target_pairs={{0,16},{16,0},{1,17},{17,1},{2,18},{18,2},{3,19},{19,3},{4,20},{20... | collective-permute-start | bytes 1572872 | tf_op jit(solution)/shard_map/ppermute | solution.py:28
  356.8 40.0 %collective-permute-start.11 = (bf16[1024,1280]{1,0:T(8,128)(2,1)}, bf16[1024,1280]{1,0:T(8,128)(2,1)}, u32[]{:S(2)}, u32[]{:S(2)}) collective-permute-start(bf16[1024,1280]{1,0:T(8,128)(2,1)} %broadcast_select_fusion.2), channel_id=1, source_target_pairs={{0,16},{16,0},{1,17},{17,1},{2,18},{18,2},{3,19},{19,3},{4,20},{20... | collective-permute-start | bytes 7864328 | tf_op jit(solution)/shard_map/ppermute | solution.py:28
  359.6 30.5 %all-to-all-start.2 = ((bf16[128,8,512]{0,2,1:T(8,128)(2,1)}), bf16[128,8,512]{0,2,1:T(8,128)(2,1)}, u32[]{:S(2)}, u32[]{:S(2)}) async-start(bf16[128,8,512]{0,2,1:T(8,128)(2,1)} %bitcast.75), calls=%async_computation.4 | async-start | bytes 2097152 | tf_op jit(solution)/shard_map/all_to_all | solution.py:33
  363.9 1.4 copy-start.4
  363.9 1.5 copy-start.6
  390.1 29.8 %all-to-all-start.1 = ((bf16[8,128,512]{2,1,0:T(8,128)(2,1)}), bf16[8,128,512]{2,1,0:T(8,128)(2,1)}, u32[]{:S(2)}, u32[]{:S(2)}) async-start(bf16[8,128,512]{2,1,0:T(8,128)(2,1)} %fusion.39), calls=%async_computation.3 | async-start | bytes 2097152 | tf_op jit(solution)/shard_map/all_to_all | solution.py:94
  396.9 2.3 copy-start.8
Sparse Core Ops, SparseCore 0:
  49.6 71.2 reduce-scatter.2
  123.7 53.5 all-gather.2
  207.9 69.5 reduce-scatter.4
  280.1 53.4 all-gather.4
